TPU v7x, 8 devices: a whole 2x2x1 slice. The times are simulated.
8 devices in a mesh: dp: 2 (over z, y), sp: 4 (over x, core).
Axes of the slice: x: 2, y: 2, z: 1, core: 2. Of those that a mesh axis runs over, the one named last changes fastest.
Arguments:
- u_in: bfloat16 [4, 1024, 4096], P('dp', 'sp'), parts along dimension 0
- w_in: bfloat16 [4096, 12288], replicated
- b_in: float32 [12288], replicated
- conv_taps: float32 [3, 12288], replicated
- w_out: bfloat16 [4096, 4096], replicated
- skip_one: float32 [4096], replicated
- skip_two: float32 [4096], replicated
- filt_one: float32 [1024, 4096], P('sp')
- filt_two: float32 [1024, 4096], P('sp')
Outputs:
- output: bfloat16 [4, 1024, 4096], P('dp', 'sp'), parts along dimension 0
There are 2 independent parts. A program takes and returns all parts, laid end to end along the dimension named above; an argument that names none is the same for every part.
All inputs are finite; a program needn't handle non-finite values.
Results may differ from a plain program's by a relative error of at most 0.014832.
Values sent between devices are 32-bit elements.
A program may use at most 1 GiB of HBM per device.

v0:
```python
import functools

import jax
import jax.numpy as jnp
import numpy as np
from jax import lax
from jax.experimental import pallas as pl
from jax.experimental.pallas import tpu as pltpu
from jax.sharding import PartitionSpec as P

F32, BF16 = jnp.float32, jnp.bfloat16
BLK = 128
TN = 512
TC = 256
N_CHUNK = 4


def split_table(table):
    parts, rest = [], table.astype(np.float64)
    for _ in range(3):
        part = rest.astype(np.float32).astype(jnp.bfloat16)
        parts.append(part)
        rest = rest - part.astype(np.float64)
    return parts


def transform_tables():
    freq = np.concatenate([np.arange(0, BLK, 2), np.arange(1, BLK, 2)]) + 0.5
    angle = 2.0 * np.pi * freq[:, None] * np.arange(BLK)[None, :] / (2 * BLK)
    fwd = np.concatenate([np.cos(angle), -np.sin(angle)], 0)
    inv = np.concatenate([np.cos(angle).T, -np.sin(angle).T], 1) / BLK
    f1, f2, f3 = split_table(fwd)
    e1, e2, e3 = split_table(inv)
    fwd3 = np.concatenate([f1, f2, f3], 1)
    fwd6 = np.concatenate([f1, f1, f2, f2, f1, f3], 1)
    inv6 = np.concatenate([e1, e1, e2, e2, e1, e3], 1)
    return fwd3, fwd6, inv6


def dot(a, b):
    return jnp.dot(a, b, preferred_element_type=F32)


def split3(x):
    hi = x.astype(BF16)
    rest = x - hi.astype(F32)
    mid = rest.astype(BF16)
    low = (rest - mid.astype(F32)).astype(BF16)
    return hi, mid, low


def stack6(hi, mid, low):
    return jnp.concatenate([hi, mid, hi, mid, low, hi], axis=0)


def short_conv(pbuf, t_ref, rows):
    return (t_ref[0:1] * pbuf[8:8 + rows] + t_ref[1:2] * pbuf[7:7 + rows] + t_ref[2:3] * pbuf[6:6 + rows]).astype(BF16)


def value_spectrum(fwd3_ref, q, dst):
    for j in range(q.shape[0] // BLK):
        blk = q[j * BLK:(j + 1) * BLK]
        dst[j] = dot(fwd3_ref[...], jnp.concatenate([blk, blk, blk], axis=0))


def in_own_body(nt, sc_ref, fwd3_ref, own_ref, pa_ref, pb_ref, pc_ref, pd_ref, tail_ref, w_ref, b_ref, t_ref, q_ref, q2_ref, vhat_ref, lhs, pbuf):
    c, on_b = sc_ref[0], sc_ref[1] == 1
    j = pl.program_id(0)
    n_seq, half = own_ref.shape[0], own_ref.shape[1]
    n_own = 2 * half
    rows = n_seq * n_own

    @pl.when(j == 0)
    def _():
        for s in range(n_seq):
            base = s * n_own
            lhs[pl.ds(pl.multiple_of(base + c * half, half), half), :] = own_ref[s]
            for h in range(2):
                piece = (pa_ref, pb_ref, pc_ref, pd_ref)[2 * s + h]
                start = base + (1 - c) * half + h * (half // 2)
                lhs[pl.ds(pl.multiple_of(start, half // 2), half // 2), :] = piece[...].astype(BF16)
        lhs[rows:, :] = tail_ref[...].astype(BF16)

    p = (dot(lhs[...], w_ref[...]) + b_ref[...]).astype(BF16).astype(F32)
    for s in range(n_seq):
        pbuf[s, 0:8] = jnp.where(on_b, p[rows + 8 * s:rows + 8 * s + 8], 0.0)
        pbuf[s, 8:] = p[s * n_own:(s + 1) * n_own]

    @pl.when(j < 2 * nt)
    def _():
        for s in range(n_seq):
            q_ref[s] = short_conv(pbuf.at[s], t_ref, n_own).reshape(q_ref.shape[1:])

    @pl.when(j >= 2 * nt)
    def _():
        for s in range(n_seq):
            q2_ref[s] = short_conv(pbuf.at[s], t_ref, n_own)

    @pl.when((j >= nt) & (j < 2 * nt))
    def _():
        for s in range(n_seq):
            value_spectrum(fwd3_ref, q_ref[s].reshape(n_own, -1), vhat_ref.at[s])


def gather_rows(sc_ref, near_ref, far_ref, lhs):
    c, rows = sc_ref[0], near_ref.shape[0]

    @pl.when(pl.program_id(0) == 0)
    def _():
        lhs[pl.ds(pl.multiple_of(c * rows, rows), rows), :] = near_ref[...].astype(BF16)
        lhs[pl.ds(pl.multiple_of((1 - c) * rows, rows), rows), :] = far_ref[...].astype(BF16)


def prev_a_body(sc_ref, near_ref, far_ref, w_ref, b_ref, p_ref, lhs):
    gather_rows(sc_ref, near_ref, far_ref, lhs)
    p_ref[...] = (dot(lhs[...], w_ref[...]) + b_ref[...]).astype(BF16)


def prev_b_body(nt, sc_ref, fwd3_ref, near_ref, far_ref, w_ref, b_ref, t_ref, pa_ref, q_in, vhat_in, q_ref, vhat_ref, lhs, pbuf):
    on_b = sc_ref[1] == 1
    rows = near_ref.shape[0]
    gather_rows(sc_ref, near_ref, far_ref, lhs)
    p = (dot(lhs[...], w_ref[...]) + b_ref[...]).astype(BF16).astype(F32)
    pbuf[0:8] = jnp.zeros((8, p.shape[1]), F32)
    for core in range(2):
        for h, piece in enumerate((pa_ref[...].astype(F32), p)):
            base = 8 + (2 * core + h) * rows
            pbuf[base:base + rows] = jnp.where(on_b, piece[core * rows:(core + 1) * rows], 0.0)
    q_ref[0] = short_conv(pbuf, t_ref, 4 * rows).reshape(q_ref.shape[1:])

    @pl.when(pl.program_id(0) >= nt)
    def _():
        value_spectrum(fwd3_ref, q_ref[0].reshape(4 * rows, -1), vhat_ref.at[0])


def split_blocks(src, parts, first):
    for j in range(src.shape[0] // BLK):
        for i, a in enumerate(split3(src[j * BLK:(j + 1) * BLK])):
            parts[first + j, i] = a


def block_spectrum(fwd6_ref, parts, j):
    return dot(fwd6_ref[...], stack6(parts[j, 0], parts[j, 1], parts[j, 2]))


def shifted_add(cur, old, lo, sign):
    re, im = slice(lo, lo + BLK // 2), slice(BLK + lo, BLK + lo + BLK // 2)
    return re, im, cur[re] - sign * old[im], cur[im] + sign * old[re]


SIDES = ((0, 1.0), (BLK // 2, -1.0))


def far_body(sc_ref, fwd6_ref, own1_ref, own2_ref, pf1_ref, pf2_ref, g_ref, parts):
    c = sc_ref[0]
    hk = own1_ref.shape[0] // BLK
    for f in range(2):
        split_blocks((own1_ref, own2_ref)[f], parts.at[f], c * hk)
        split_blocks((pf1_ref, pf2_ref)[f], parts.at[f], (1 - c) * hk)
        for j in range(2 * hk):
            g_ref[f, j] = block_spectrum(fwd6_ref, parts.at[f], j)
        for j in range(2 * hk - 1, 0, -1):
            for lo, sign in SIDES:
                re, im, new_re, new_im = shifted_add(g_ref.at[f, j], g_ref.at[f, j - 1], lo, sign)
                g_ref[f, j, re], g_ref[f, j, im] = new_re, new_im


def out_body(n_chunk, sc_ref, *refs):
    keeps, parts = refs[:n_chunk], refs[n_chunk:2 * n_chunk]
    wk_ref, wp_ref, u_ref, o_ref, lhs_k, lhs_p = refs[2 * n_chunk:]

    @pl.when(pl.program_id(0) == 0)
    def _():
        n_seq, n_pos, nch = keeps[0].shape
        for i in range(n_chunk):
            cols = slice(i * nch, (i + 1) * nch)
            lhs_k[:, cols] = keeps[i][...].reshape(n_seq * n_pos, nch)
            lhs_p[:, cols] = parts[i][...].reshape(n_seq * n_pos, nch).astype(BF16)

    acc = dot(lhs_k[...], wk_ref[...]) + dot(lhs_p[...], wp_ref[...])
    o_ref[...] = (u_ref[...].astype(F32) + acc.reshape(o_ref.shape)).astype(BF16)


def conv_body(sc_ref, fwd6_ref, inv6_ref, x1_ref, v_ref, x2_ref, vhat, far_ref, sk1_ref, sk2_ref,
              own1_ref, own2_ref, pf1_ref, pf2_ref, xs_ref, xc_ref, ys_ref, yc_ref,
              keep_ref, send_ref, hparts, g1, g2, sp0, sp1, zp0, zp1, zv0, zv1, zh0, zh1, ybuf):
    c, on_b, d = sc_ref[0], sc_ref[1] == 1, sc_ref[2]
    n_seq, nb = vhat.shape[0], vhat.shape[1]
    nbo = nb // 2
    hk = own1_ref.shape[0] // BLK
    g, sparts, zparts, zval, zhat = (g1, g2), (sp0, sp1), (zp0, zp1), (zv0, zv1), (zh0, zh1)

    @pl.when(on_b)
    def _():
        for ref, f, side in ((xs_ref, d, c), (xc_ref, d, 1 - c), (ys_ref, 1 - d, c), (yc_ref, 1 - d, 1 - c)):
            split_blocks(ref, hparts.at[f], side * hk)

    @pl.when(jnp.logical_not(on_b))
    def _():
        for ref, f, side in ((own1_ref, 0, c), (pf1_ref, 0, 1 - c), (own2_ref, 1, c), (pf2_ref, 1, 1 - c)):
            split_blocks(ref, hparts.at[f], side * hk)

    def near_spectrum(f, j):
        g[f][j] = block_spectrum(fwd6_ref, hparts.at[f], j)

    def window(f):
        for j in range(nbo, 0, -1):
            cur = far_ref.at[f, 0] if j == nbo else g[f].at[j]
            for lo, sign in SIDES:
                re, im, new_re, new_im = shifted_add(cur, g[f].at[j - 1], lo, sign)
                g[f][j, re], g[f][j, im] = new_re, new_im

    def pointwise(xhat, f, dst, r, first):
        re, im = pl.ds(pl.multiple_of(r * 16, 16), 16), pl.ds(pl.multiple_of(BLK + r * 16, 16), 16)
        for k in range(first, nb):
            acc_re = acc_im = None
            for j in range(k + 1):
                i = k - j
                gr, gi = (g[f][i, re], g[f][i, im]) if i <= nbo else (far_ref[f, i - nbo, re], far_ref[f, i - nbo, im])
                xr, xi = xhat[j, re], xhat[j, im]
                t_re, t_im = xr * gr - xi * gi, xr * gi + xi * gr
                acc_re = t_re if acc_re is None else acc_re + t_re
                acc_im = t_im if acc_im is None else acc_im + t_im
            for part, (a, b) in enumerate(zip(split3(acc_re), split3(acc_im))):
                dst[k, part, re], dst[k, part, im] = a, b

    def inverse(s, k):
        return dot(inv6_ref[...], stack6(sparts[s][k, 0], sparts[s][k, 1], sparts[s][k, 2]))

    def gate_one(s, k):
        z = x1_ref[s, k].astype(F32) * (inverse(s, k) + sk1_ref[...] * v_ref[s, k].astype(F32))
        zval[s][k] = z
        for part, a in enumerate(split3(z)):
            zparts[s][k, part] = a

    def spectrum(s, k):
        zhat[s][k] = block_spectrum(fwd6_ref, zparts[s], k)

    def gate_two(s, k):
        y = x2_ref[s, k].astype(F32) * (inverse(s, nbo + k) + sk2_ref[...] * zval[s][nbo + k])
        ybuf[s, k] = y.astype(BF16)

    def loop(body, trips=nb // 2):
        def run(i, carry):
            body(i)
            return carry

        lax.fori_loop(0, trips, run, 0)

    for j in range(nbo):
        near_spectrum(0, j)
    window(0)

    @loop
    def _(i):
        pointwise(vhat.at[0], 0, sparts[0], 2 * i, 0)
        near_spectrum(1, i)
        pointwise(vhat.at[0], 0, sparts[0], 2 * i + 1, 0)

    window(1)

    @loop
    def _(i):
        for r in range(2):
            pointwise(vhat.at[1], 0, sparts[1], 2 * i + r, 0)
            gate_one(0, 2 * i + r)

    @functools.partial(loop, trips=nb // 4)
    def _(i):
        for r in range(4):
            gate_one(1, 4 * i + r)
            spectrum(0, 4 * i + r)

    @loop
    def _(i):
        for r in range(2):
            pointwise(zhat[0], 1, sparts[0], 2 * i + r, nbo)
            spectrum(1, 2 * i + r)

    @functools.partial(loop, trips=nbo // 2)
    def _(i):
        for r in range(4):
            pointwise(zhat[1], 1, sparts[1], 4 * i + r, nbo)
            if r % 2:
                gate_two(0, 2 * i + r // 2)

    for k in range(nbo):
        gate_two(1, k)

    for s in range(n_seq):
        for b in range(hk):
            keep_ref[s, b * BLK:(b + 1) * BLK] = ybuf[s, c * hk + b]
            send_ref[s, b * BLK:(b + 1) * BLK] = ybuf[s, (1 - c) * hk + b].astype(F32)


def params(mib=60):
    return pltpu.CompilerParams(vmem_limit_bytes=mib << 20, dimension_semantics=("arbitrary",))


def cost(flops, nbytes):
    return pl.CostEstimate(flops=int(flops), bytes_accessed=int(nbytes), transcendentals=0)


def solution(mesh):
    n_sp = mesh.shape["sp"]
    half_sp = n_sp // 2
    partner = [(i, i ^ 1) for i in range(n_sp)]
    over_same = [(i, i + half_sp) for i in range(half_sp)]
    over_cross = [(i, (i ^ 1) + half_sp) for i in range(half_sp)]
    swap_dp = [(0, 1), (1, 0)]
    fwd3, fwd6, inv6 = transform_tables()

    def hop(x, perm, axis="sp"):
        return lax.ppermute(x, axis, perm)

    def compute(u_in, w_in, b_in, conv_taps, w_out, skip_one, skip_two, filt_one, filt_two):
        sp, dp = lax.axis_index("sp"), lax.axis_index("dp")
        c = sp % 2
        scalars = jnp.stack([c, (sp >= half_sp).astype(jnp.int32), dp]).astype(jnp.int32)
        n_seq, n_pos, width = u_in.shape
        half_w = width // 2
        n_own = 2 * n_pos
        nb = 2 * n_own // BLK
        nbo = nb // 2

        hp = n_pos // 2
        pieces, gate = [], u_in[0, 0, :128].astype(F32)
        for s in range(n_seq):
            for h in range(2):
                raw, gate = lax.optimization_barrier((u_in[s, h * hp:(h + 1) * hp], gate))
                pieces.append(raw.astype(F32))
                gate = pieces[-1]
        over = [hop(x, over_same) for x in pieces]
        over_part = [hop(x, partner) for x in over]
        u_part = [hop(x, partner) for x in pieces]
        tail = jnp.concatenate([pieces[2 * s + 1][-8:] for s in range(n_seq)], axis=0)
        u_tail = hop(tail, [(half_sp - 1, half_sp)]) + hop(tail, [(half_sp - 1, half_sp + 1)])

        mine, other = c * half_w, (1 - c) * half_w

        def chan_half(f, start):
            return lax.dynamic_slice(f, (0, start), (n_pos, half_w))

        f_part = [hop(chan_half(f, other), partner) for f in (filt_one, filt_two)]
        f_link = jnp.where(dp == 0, filt_one, filt_two)
        f_mine, f_other = chan_half(f_link, mine), chan_half(f_link, other)
        nch = half_w // N_CHUNK
        near = []
        for j in range(N_CHUNK):
            cols = slice(j * nch, (j + 1) * nch)
            xs, xc = hop(f_mine[:, cols], over_same), hop(f_other[:, cols], over_cross)
            ys, yc = hop(xs, swap_dp, "dp"), hop(xc, swap_dp, "dp")
            near.append((xs, xc, ys, yc))

        bias = b_in.reshape(1, -1)
        nt = half_w // TN
        wt = width // TN
        any_spec = pl.BlockSpec(memory_space=pl.ANY)

        def fixed(shape):
            return pl.BlockSpec(shape, lambda *a: (0,) * len(shape))

        def own_col(j, sc):
            group = jnp.where(j < nt, 0, jnp.where(j < 2 * nt, 2, 1))
            return (0, group * wt + sc[0] * nt + j % nt)

        q_shape = jax.ShapeDtypeStruct((n_seq, nb, BLK, width), BF16)
        vhat_shape = jax.ShapeDtypeStruct((n_seq, nb, 2 * BLK, half_w), F32)
        q, q2, vhat = pl.pallas_call(
            functools.partial(in_own_body, nt),
            grid_spec=pltpu.PrefetchScalarGridSpec(
                num_scalar_prefetch=1,
                grid=(3 * nt,),
                in_specs=[
                    fixed(fwd3.shape),
                    fixed((n_seq, n_pos, width)),
                    *[fixed((hp, width))] * 4,
                    fixed((16, width)),
                    pl.BlockSpec((width, TN), own_col),
                    pl.BlockSpec((1, TN), own_col),
                    pl.BlockSpec((3, TN), own_col),
                ],
                out_specs=[
                    pl.BlockSpec((n_seq, nbo, BLK, TN), lambda j, sc: (0, 1, 0, jnp.minimum(j, 2 * nt - 1))),
                    pl.BlockSpec((n_seq, n_own, TN), lambda j, sc: (0, 0, jnp.maximum(j - 2 * nt, 0))),
                    pl.BlockSpec((n_seq, nbo, 2 * BLK, TN), lambda j, sc: (0, 1, 0, jnp.clip(j - nt, 0, nt - 1))),
                ],
                scratch_shapes=[pltpu.VMEM((n_seq * n_own + 16, width), BF16), pltpu.VMEM((n_seq, n_own + 8, TN), F32)],
            ),
            out_shape=[q_shape, jax.ShapeDtypeStruct((n_seq, n_own, half_w), BF16), vhat_shape],
            compiler_params=params(),
            cost_estimate=cost(2 * n_seq * n_own * width * 3 * half_w, 2 * width * 3 * half_w),
            name="in_own",
        )(scalars, fwd3, u_in, *u_part, u_tail, w_in, bias, conv_taps)

        def prev_col(j, sc):
            return (0, jnp.where(j < nt, 0, 2) * wt + sc[0] * nt + j % nt)

        def prev_a(i):
            return pl.pallas_call(
                prev_a_body,
                grid_spec=pltpu.PrefetchScalarGridSpec(
                    num_scalar_prefetch=1,
                    grid=(2 * nt,),
                    in_specs=[
                        fixed((hp, width)),
                        fixed((hp, width)),
                        pl.BlockSpec((width, TN), prev_col),
                        pl.BlockSpec((1, TN), prev_col),
                    ],
                    out_specs=pl.BlockSpec((n_pos, TN), lambda j, sc: (0, j)),
                    scratch_shapes=[pltpu.VMEM((n_pos, width), BF16)],
                ),
                out_shape=jax.ShapeDtypeStruct((n_pos, width), BF16),
                compiler_params=params(),
                cost_estimate=cost(2 * n_pos * width * width, 2 * width * width),
                name="prev_a",
            )(scalars, over[i], over_part[i], w_in, bias)

        def prev_b(s, pa, q, vhat):
            i = 2 * s + 1
            return pl.pallas_call(
                functools.partial(prev_b_body, nt),
                grid_spec=pltpu.PrefetchScalarGridSpec(
                    num_scalar_prefetch=1,
                    grid=(2 * nt,),
                    in_specs=[
                        fixed(fwd3.shape),
                        fixed((hp, width)),
                        fixed((hp, width)),
                        pl.BlockSpec((width, TN), prev_col),
                        pl.BlockSpec((1, TN), prev_col),
                        pl.BlockSpec((3, TN), prev_col),
                        pl.BlockSpec((n_pos, TN), lambda j, sc: (0, j)),
                        any_spec,
                        any_spec,
                    ],
                    out_specs=[
                        pl.BlockSpec((1, nbo, BLK, TN), lambda j, sc: (s, 0, 0, j)),
                        pl.BlockSpec((1, nbo, 2 * BLK, TN), lambda j, sc: (s, 0, 0, jnp.maximum(j - nt, 0))),
                    ],
                    scratch_shapes=[pltpu.VMEM((n_pos, width), BF16), pltpu.VMEM((n_own + 8, TN), F32)],
                ),
                out_shape=[q_shape, vhat_shape],
                input_output_aliases={8: 0, 9: 1},
                compiler_params=params(),
                cost_estimate=cost(2 * n_pos * width * width, 2 * width * width),
                name="prev_b",
            )(scalars, fwd3, over[i], over_part[i], w_in, bias, conv_taps, pa, q, vhat)

        for s in range(n_seq):
            pa = prev_a(2 * s)
            q, vhat = prev_b(s, pa, q, vhat)

        tf = TN
        far = pl.pallas_call(
            far_body,
            grid_spec=pltpu.PrefetchScalarGridSpec(
                num_scalar_prefetch=1,
                grid=(half_w // tf,),
                in_specs=[
                    fixed(fwd6.shape),
                    pl.BlockSpec((n_pos, tf), lambda j, sc: (0, sc[0] * (half_w // tf) + j)),
                    pl.BlockSpec((n_pos, tf), lambda j, sc: (0, sc[0] * (half_w // tf) + j)),
                    pl.BlockSpec((n_pos, tf), lambda j, sc: (0, j)),
                    pl.BlockSpec((n_pos, tf), lambda j, sc: (0, j)),
                ],
                out_specs=pl.BlockSpec((2, nbo, 2 * BLK, tf), lambda j, sc: (0, 0, 0, j)),
                scratch_shapes=[pltpu.VMEM((2, nbo, 3, BLK, tf), BF16)],
            ),
            out_shape=jax.ShapeDtypeStruct((2, nbo, 2 * BLK, half_w), F32),
            compiler_params=params(),
            cost_estimate=cost(6e9, 3e7),
            name="far_spectrum",
        )(scalars, fwd6, filt_one, filt_two, *f_part)

        tiles = nch // TC
        ht = half_w // TC
        q2 = q2.reshape(n_seq, nbo, BLK, half_w)

        def conv(j, xs, xc, ys, yc):
            base = j * tiles

            def col4(shape, first):
                return pl.BlockSpec(shape + (TC,), lambda t, sc: (0, 0, 0, first + base + t))

            chan = pl.BlockSpec((1, TC), lambda t, sc: (0, sc[0] * ht + base + t))
            own_f = pl.BlockSpec((n_pos, TC), lambda t, sc: (0, sc[0] * ht + base + t))
            part_f = pl.BlockSpec((n_pos, TC), lambda t, sc: (0, base + t))
            local = pl.BlockSpec((n_pos, TC), lambda t, sc: (0, t))
            return pl.pallas_call(
                conv_body,
                grid_spec=pltpu.PrefetchScalarGridSpec(
                    num_scalar_prefetch=1,
                    grid=(tiles,),
                    in_specs=[
                        fixed(fwd6.shape), fixed(inv6.shape),
                        col4((n_seq, nb, BLK), 0), col4((n_seq, nb, BLK), ht), col4((n_seq, nbo, BLK), 0),
                        col4((n_seq, nb, 2 * BLK), 0), col4((2, nbo, 2 * BLK), 0),
                        chan, chan, own_f, own_f,
                        part_f, part_f, local, local, local, local,
                    ],
                    out_specs=[pl.BlockSpec((n_seq, n_pos, TC), lambda t, sc: (0, 0, t))] * 2,
                    scratch_shapes=[
                        pltpu.VMEM((2, nbo, 3, BLK, TC), BF16),
                        *[pltpu.VMEM((nbo + 1, 2 * BLK, TC), F32)] * 2,
                        *[pltpu.VMEM((nb, 3, 2 * BLK, TC), BF16)] * n_seq,
                        *[pltpu.VMEM((nb, 3, BLK, TC), BF16)] * n_seq,
                        *[pltpu.VMEM((nb, BLK, TC), F32)] * n_seq,
                        *[pltpu.VMEM((nb, 2 * BLK, TC), F32)] * n_seq,
                        pltpu.VMEM((n_seq, nbo, BLK, TC), BF16),
                    ],
                ),
                out_shape=[jax.ShapeDtypeStruct((n_seq, n_pos, nch), BF16), jax.ShapeDtypeStruct((n_seq, n_pos, nch), F32)],
                compiler_params=params(),
                cost_estimate=cost(24e9 / N_CHUNK, 8e7 / N_CHUNK),
                name="long_conv",
            )(scalars, fwd6, inv6, q, q, q2, vhat, far, skip_one.reshape(1, -1), skip_two.reshape(1, -1),
              filt_one, filt_two, *f_part, xs, xc, ys, yc)

        keeps, parts = [], []
        for j in range(N_CHUNK):
            keep, send = conv(j, *near[j])
            keeps.append(keep)
            parts.append(hop(send, partner))
        return pl.pallas_call(
            functools.partial(out_body, N_CHUNK),
            grid_spec=pltpu.PrefetchScalarGridSpec(
                num_scalar_prefetch=1,
                grid=(wt,),
                in_specs=[
                    *[fixed((n_seq, n_pos, nch))] * (2 * N_CHUNK),
                    pl.BlockSpec((half_w, TN), lambda j, sc: (sc[0], j)),
                    pl.BlockSpec((half_w, TN), lambda j, sc: (1 - sc[0], j)),
                    pl.BlockSpec((n_seq, n_pos, TN), lambda j, sc: (0, 0, j)),
                ],
                out_specs=pl.BlockSpec((n_seq, n_pos, TN), lambda j, sc: (0, 0, j)),
                scratch_shapes=[pltpu.VMEM((n_seq * n_pos, half_w), BF16)] * 2,
            ),
            out_shape=jax.ShapeDtypeStruct((n_seq, n_pos, width), BF16),
            compiler_params=params(),
            cost_estimate=cost(2 * n_seq * n_pos * width * width, 2 * width * width),
            name="out_proj",
        )(scalars, *keeps, *parts, w_out, w_out, u_in)

    seq_spec = P("dp", "sp", None)
    filt_spec = P("sp", None)
    return jax.shard_map(compute, mesh=mesh, in_specs=(seq_spec, P(), P(), P(), P(), P(), P(), filt_spec, filt_spec), out_specs=seq_spec, check_vma=False)
```

profile of v0, /device:TPU:0, one launch (start us, length us, event | category | flops | bytes accessed | tf_op | source)
XLA Modules:
  0.0 518.4 jit_solution(10933485728200989212)
XLA Ops:
  0.0 2.7 slice_bitcast_fusion
  11.2 5.0 collective-permute-start.9
  16.2 1.9 collective-permute-start.8
  18.1 5.6 %collective-permute-start.6 = (f32[128,4096]{1,0:T(8,128)}, f32[128,4096]{1,0:T(8,128)}, u32[]{:S(2)}, u32[]{:S(2)}) collective-permute-start(f32[128,4096]{1,0:T(8,128)} %convert_element_type.14), channel_id=1, source_target_pairs={{0,2},{1,3},{4,6},{5,7}} | collective-permute-start | bytes 6291464 | tf_op jit(solution)/shard_map/ppermute | solution.py:314
  23.8 2.7 collective-permute-start.4
  26.4 2.6 collective-permute-start.2
  29.7 2.7 broadcast_select_fusion
  32.4 2.2 constant_dynamic-slice_fusion.6
  41.3 2.6 collective-permute-start
  43.9 2.3 collective-permute-start.14
  46.2 20.8 %collective-permute-done.6.near_ref = f32[128,4096]{1,0:T(8,128)} collective-permute-done((f32[128,4096]{1,0:T(8,128)}, f32[128,4096]{1,0:T(8,128)}, u32[]{:S(2)}, u32[]{:S(2)}) %collective-permute-start.6) | collective-permute-done | bytes 2097184 | tf_op jit(solution)/shard_map/ppermute | solution.py:314
  67.1 3.4 collective-permute-start.15
  70.5 41.5 %collective-permute-done.4.near_ref = f32[128,4096]{1,0:T(8,128)} collective-permute-done((f32[128,4096]{1,0:T(8,128)}, f32[128,4096]{1,0:T(8,128)}, u32[]{:S(2)}, u32[]{:S(2)}) %collective-permute-start.4) | collective-permute-done | bytes 2097184 | tf_op jit(solution)/shard_map/ppermute | solution.py:314
  112.0 3.4 collective-permute-start.7
  115.4 41.5 %collective-permute-done.2.near_ref = f32[128,4096]{1,0:T(8,128)} collective-permute-done((f32[128,4096]{1,0:T(8,128)}, f32[128,4096]{1,0:T(8,128)}, u32[]{:S(2)}, u32[]{:S(2)}) %collective-permute-start.2) | collective-permute-done | bytes 2097184 | tf_op jit(solution)/shard_map/ppermute | solution.py:314
  156.9 3.4 collective-permute-start.3
  160.4 79.7 %in_own.1 = (bf16[2,8,128,4096]{3,2,1,0:T(8,128)(2,1)}, bf16[2,512,2048]{2,1,0:T(8,128)(2,1)}, f32[2,8,256,2048]{3,2,1,0:T(8,128)}) custom-call(s32[3]{0:T(128)} %pad_add_fusion.sc_ref, bf16[256,384]{1,0:T(8,128)(2,1)} %constant.34.clone.fwd3_ref, bf16[2,256,4096]{2,1,0:T(8,128)(2,1)} %refs_10_.1, f32[128,4096]{1,0:T(8,128)} %collective-permute-done.8.pa_ref, ...), custom_call_target="tpu_custom_call" | custom-call | flops 51539607552 | bytes 50331648 | tf_op jit(solution)/shard_map/in_own/pallas_call | solution.py:369
  240.1 5.2 %collective-permute-start.28 = (f32[256,512]{1,0:T(8,128)}, f32[256,512]{1,0:T(8,128)}, u32[]{:S(2)}, u32[]{:S(2)}) collective-permute-start(f32[256,512]{1,0:T(8,128)} %get-tuple-element.48), channel_id=1, source_target_pairs={{0,2},{1,3},{4,6},{5,7}} | collective-permute-start | bytes 1572872 | tf_op jit(solution)/shard_map/ppermute | solution.py:314
  245.3 15.4 %far_spectrum.1.far_ref = f32[2,4,256,2048]{3,2,1,0:T(8,128)} custom-call(s32[3]{0:T(128)} %pad_add_fusion.sc_ref, bf16[256,768]{1,0:T(8,128)(2,1)} %constant.35.clone.fwd6_ref, f32[256,4096]{1,0:T(8,128)} %own1_ref.9, f32[256,4096]{1,0:T(8,128)} %own2_ref.9, f32[256,2048]{1,0:T(8,128)} %copy-done.2, f32[256,2048]{1,0:T(8,128)} %collective-permute-done.15.pf2_ref), custom_call_target="tpu_custom_call" | custom-call | flops 6000000000 | bytes 30000000 | tf_op jit(solution)/shard_map/far_spectrum/pallas_call | solution.py:456
  260.7 2.1 collective-permute-start.29
  263.3 19.0 %prev_a.3.pa_ref = bf16[256,4096]{1,0:T(8,128)(2,1)} custom-call(s32[3]{0:T(128)} %pad_add_fusion.sc_ref, f32[128,4096]{1,0:T(8,128)} %collective-permute-done.6.near_ref, f32[128,4096]{1,0:T(8,128)} %collective-permute-done.7.far_ref, bf16[4096,12288]{1,0:T(8,128)(2,1)} %w_ref.9, f32[1,12288]{1,0:T(1,128)} %bitcast.20), custom_call_target="tpu_custom_call" | custom-call | flops 8589934592 | bytes 33554432 | tf_op jit(solution)/shard_map/prev_a/pallas_call | solution.py:400
  282.4 11.7 %collective-permute-start.24 = (f32[256,512]{1,0:T(8,128)}, f32[256,512]{1,0:T(8,128)S(1)}, u32[]{:S(2)}, u32[]{:S(2)}) collective-permute-start(f32[256,512]{1,0:T(8,128)} %get-tuple-element.43), channel_id=1, source_target_pairs={{0,2},{1,3},{4,6},{5,7}} | collective-permute-start | bytes 1572872 | tf_op jit(solution)/shard_map/ppermute | solution.py:314
  294.1 19.1 %prev_a.2.pa_ref = bf16[256,4096]{1,0:T(8,128)(2,1)} custom-call(s32[3]{0:T(128)} %pad_add_fusion.sc_ref, f32[128,4096]{1,0:T(8,128)} %collective-permute-done.2.near_ref, f32[128,4096]{1,0:T(8,128)} %collective-permute-done.3.far_ref, bf16[4096,12288]{1,0:T(8,128)(2,1)} %w_ref.9, f32[1,12288]{1,0:T(1,128)} %bitcast.21), custom_call_target="tpu_custom_call" | custom-call | flops 8589934592 | bytes 33554432 | tf_op jit(solution)/shard_map/prev_a/pallas_call | solution.py:400
  314.5 24.4 %prev_b.2 = (bf16[2,8,128,4096]{3,2,1,0:T(8,128)(2,1)}, f32[2,8,256,2048]{3,2,1,0:T(8,128)}) custom-call(s32[3]{0:T(128)} %pad_add_fusion.sc_ref, bf16[256,384]{1,0:T(8,128)(2,1)} %constant.34.clone.fwd3_ref, f32[128,4096]{1,0:T(8,128)} %collective-permute-done.4.near_ref, ...), custom_call_target="tpu_custom_call", output_to_operand_aliasing={{0}: (8, {}), {1}: (9, {})} | custom-call | flops 8589934592 | bytes 33554432 | tf_op jit(solution)/shard_map/prev_b/pallas_call | solution.py:422
  343.2 24.4 %prev_b.3 = (bf16[2,8,128,4096]{3,2,1,0:T(8,128)(2,1)}, f32[2,8,256,2048]{3,2,1,0:T(8,128)}) custom-call(s32[3]{0:T(128)} %pad_add_fusion.sc_ref, bf16[256,384]{1,0:T(8,128)(2,1)} %constant.34.clone.fwd3_ref, f32[128,4096]{1,0:T(8,128)} %collective-permute-done.near_ref, f32[128,4096]{1,0:T(8,128)} %copy-done.3, ...), custom_call_target="tpu_custom_call", output_to_operand_aliasing={{0}: (8, {}), {1}: (9, {})} | custom-call | flops 8589934592 | bytes 33554432 | tf_op jit(solution)/shard_map/prev_b/pallas_call | solution.py:422
  370.3 2.1 collective-permute-start.17
  374.5 27.2 %long_conv.7 = (bf16[2,256,512]{2,1,0:T(8,128)(2,1)}, f32[2,256,512]{2,1,0:T(8,128)}) custom-call(s32[3]{0:T(128)} %pad_add_fusion.sc_ref, bf16[256,768]{1,0:T(8,128)(2,1)} %constant.35.clone.fwd6_ref, bf16[128,1536]{1,0:T(8,128)(2,1)} %constant.36.clone.inv6_ref, bf16[2,8,128,4096]{3,2,1,0:T(8,128)(2,1)} %get-tuple-element.30.x1_ref.v_ref, ...), custom_call_target="tpu_custom_call" | custom-call | flops 6000000000 | bytes 20000000 | tf_op jit(solution)/shard_map/long_conv/pallas_call | solution.py:491
  406.6 27.1 %long_conv.6 = (bf16[2,256,512]{2,1,0:T(8,128)(2,1)}, f32[2,256,512]{2,1,0:T(8,128)}) custom-call(s32[3]{0:T(128)} %pad_add_fusion.sc_ref, bf16[256,768]{1,0:T(8,128)(2,1)} %constant.35.clone.fwd6_ref, bf16[128,1536]{1,0:T(8,128)(2,1)} %constant.36.clone.inv6_ref, bf16[2,8,128,4096]{3,2,1,0:T(8,128)(2,1)} %get-tuple-element.30.x1_ref.v_ref, ...), custom_call_target="tpu_custom_call" | custom-call | flops 6000000000 | bytes 20000000 | tf_op jit(solution)/shard_map/long_conv/pallas_call | solution.py:491
  433.9 27.4 %long_conv.5 = (bf16[2,256,512]{2,1,0:T(8,128)(2,1)}, f32[2,256,512]{2,1,0:T(8,128)}) custom-call(s32[3]{0:T(128)} %pad_add_fusion.sc_ref, bf16[256,768]{1,0:T(8,128)(2,1)} %constant.35.clone.fwd6_ref, bf16[128,1536]{1,0:T(8,128)(2,1)} %constant.36.clone.inv6_ref, bf16[2,8,128,4096]{3,2,1,0:T(8,128)(2,1)} %get-tuple-element.30.x1_ref.v_ref, ...), custom_call_target="tpu_custom_call" | custom-call | flops 6000000000 | bytes 20000000 | tf_op jit(solution)/shard_map/long_conv/pallas_call | solution.py:491
  461.8 27.2 %long_conv.4 = (bf16[2,256,512]{2,1,0:T(8,128)(2,1)}, f32[2,256,512]{2,1,0:T(8,128)}) custom-call(s32[3]{0:T(128)} %pad_add_fusion.sc_ref, bf16[256,768]{1,0:T(8,128)(2,1)} %constant.35.clone.fwd6_ref, bf16[128,1536]{1,0:T(8,128)(2,1)} %constant.36.clone.inv6_ref, bf16[2,8,128,4096]{3,2,1,0:T(8,128)(2,1)} %get-tuple-element.30.x1_ref.v_ref, ...), custom_call_target="tpu_custom_call" | custom-call | flops 6000000000 | bytes 20000000 | tf_op jit(solution)/shard_map/long_conv/pallas_call | solution.py:491
  489.1 2.9 collective-permute-done.32.refs_4_
  492.0 26.0 %out_proj.1 = bf16[2,256,4096]{2,1,0:T(8,128)(2,1)} custom-call(s32[3]{0:T(128)} %pad_add_fusion.sc_ref, bf16[2,256,512]{2,1,0:T(8,128)(2,1)} %get-tuple-element.33.refs_0_, bf16[2,256,512]{2,1,0:T(8,128)(2,1)} %get-tuple-element.34.refs_1_, bf16[2,256,512]{2,1,0:T(8,128)(2,1)} %get-tuple-element.35.refs_2_, bf16[2,256,512]{2,1,0:T(8,128)(2,1)} %get-tuple-element.36.refs_3_, ...), custom_call_target="tpu_custom_call" | custom-call | flops 17179869184 | bytes 33554432 | tf_op jit(solution)/shard_map/out_proj/pallas_call | solution.py:526
  (95 shorter events, 32.2 us)
Async XLA Ops:
  9.7 16.7 %collective-permute-start.10 = (f32[128,4096]{1,0:T(8,128)}, f32[128,4096]{1,0:T(8,128)}, u32[]{:S(2)}, u32[]{:S(2)}) collective-permute-start(f32[128,4096]{1,0:T(8,128)} %convert_element_type.16), channel_id=1, source_target_pairs={{0,1},{1,0},{2,3},{3,2},{4,5},{5,4},{6,7},{7,6}} | collective-permute-start | bytes 6291464 | tf_op jit(solution)/shard_map/ppermute | solution.py:314
  11.2 30.1 %collective-permute-start.9 = (f32[128,4096]{1,0:T(8,128)}, f32[128,4096]{1,0:T(8,128)}, u32[]{:S(2)}, u32[]{:S(2)}) collective-permute-start(f32[128,4096]{1,0:T(8,128)} %convert_element_type.15), channel_id=1, source_target_pairs={{0,1},{1,0},{2,3},{3,2},{4,5},{5,4},{6,7},{7,6}} | collective-permute-start | bytes 6291464 | tf_op jit(solution)/shard_map/ppermute | solution.py:314
  16.2 27.7 %collective-permute-start.8 = (f32[128,4096]{1,0:T(8,128)}, f32[128,4096]{1,0:T(8,128)}, u32[]{:S(2)}, u32[]{:S(2)}) collective-permute-start(f32[128,4096]{1,0:T(8,128)} %convert_element_type.14), channel_id=1, source_target_pairs={{0,1},{1,0},{2,3},{3,2},{4,5},{5,4},{6,7},{7,6}} | collective-permute-start | bytes 6291464 | tf_op jit(solution)/shard_map/ppermute | solution.py:314
  18.1 48.9 %collective-permute-start.6 = (f32[128,4096]{1,0:T(8,128)}, f32[128,4096]{1,0:T(8,128)}, u32[]{:S(2)}, u32[]{:S(2)}) collective-permute-start(f32[128,4096]{1,0:T(8,128)} %convert_element_type.14), channel_id=1, source_target_pairs={{0,2},{1,3},{4,6},{5,7}} | collective-permute-start | bytes 6291464 | tf_op jit(solution)/shard_map/ppermute | solution.py:314
  23.8 88.2 %collective-permute-start.4 = (f32[128,4096]{1,0:T(8,128)}, f32[128,4096]{1,0:T(8,128)}, u32[]{:S(2)}, u32[]{:S(2)}) collective-permute-start(f32[128,4096]{1,0:T(8,128)} %convert_element_type.15), channel_id=1, source_target_pairs={{0,2},{1,3},{4,6},{5,7}} | collective-permute-start | bytes 6291464 | tf_op jit(solution)/shard_map/ppermute | solution.py:314
  26.4 130.5 %collective-permute-start.2 = (f32[128,4096]{1,0:T(8,128)}, f32[128,4096]{1,0:T(8,128)}, u32[]{:S(2)}, u32[]{:S(2)}) collective-permute-start(f32[128,4096]{1,0:T(8,128)} %convert_element_type.16), channel_id=1, source_target_pairs={{0,2},{1,3},{4,6},{5,7}} | collective-permute-start | bytes 6291464 | tf_op jit(solution)/shard_map/ppermute | solution.py:314
  41.3 219.4 %collective-permute-start = (f32[128,4096]{1,0:T(8,128)}, f32[128,4096]{1,0:T(8,128)}, u32[]{:S(2)}, u32[]{:S(2)}) collective-permute-start(f32[128,4096]{1,0:T(8,128)} %convert_element_type.17), channel_id=1, source_target_pairs={{0,2},{1,3},{4,6},{5,7}} | collective-permute-start | bytes 6291464 | tf_op jit(solution)/shard_map/ppermute | solution.py:314
  43.9 196.2 %collective-permute-start.14 = (f32[256,2048]{1,0:T(8,128)}, f32[256,2048]{1,0:T(8,128)S(1)}, u32[]{:S(2)}, u32[]{:S(2)}) collective-permute-start(f32[256,2048]{1,0:T(8,128)} %constant_dynamic-slice_fusion.9), channel_id=1, source_target_pairs={{0,1},{1,0},{2,3},{3,2},{4,5},{5,4},{6,7},{7,6}} | collective-permute-start | bytes 6291464 | tf_op jit(solution)/shard_map/ppermute | solution.py:314
  67.1 178.2 %collective-permute-start.15 = (f32[256,2048]{1,0:T(8,128)}, f32[256,2048]{1,0:T(8,128)}, u32[]{:S(2)}, u32[]{:S(2)}) collective-permute-start(f32[256,2048]{1,0:T(8,128)} %constant_dynamic-slice_fusion.8), channel_id=1, source_target_pairs={{0,1},{1,0},{2,3},{3,2},{4,5},{5,4},{6,7},{7,6}} | collective-permute-start | bytes 6291464 | tf_op jit(solution)/shard_map/ppermute | solution.py:314
  112.0 150.8 %collective-permute-start.7 = (f32[128,4096]{1,0:T(8,128)}, f32[128,4096]{1,0:T(8,128)}, u32[]{:S(2)}, u32[]{:S(2)}) collective-permute-start(f32[128,4096]{1,0:T(8,128)} %collective-permute-done.6.near_ref), channel_id=1, source_target_pairs={{0,1},{1,0},{2,3},{3,2},{4,5},{5,4},{6,7},{7,6}} | collective-permute-start | bytes 6291464 | tf_op jit(solution)/shard_map/ppermute | solution.py:314
  156.9 125.4 %collective-permute-start.3 = (f32[128,4096]{1,0:T(8,128)}, f32[128,4096]{1,0:T(8,128)}, u32[]{:S(2)}, u32[]{:S(2)}) collective-permute-start(f32[128,4096]{1,0:T(8,128)} %collective-permute-done.2.near_ref), channel_id=1, source_target_pairs={{0,1},{1,0},{2,3},{3,2},{4,5},{5,4},{6,7},{7,6}} | collective-permute-start | bytes 6291464 | tf_op jit(solution)/shard_map/ppermute | solution.py:314
  240.1 98.9 %collective-permute-start.28 = (f32[256,512]{1,0:T(8,128)}, f32[256,512]{1,0:T(8,128)}, u32[]{:S(2)}, u32[]{:S(2)}) collective-permute-start(f32[256,512]{1,0:T(8,128)} %get-tuple-element.48), channel_id=1, source_target_pairs={{0,2},{1,3},{4,6},{5,7}} | collective-permute-start | bytes 1572872 | tf_op jit(solution)/shard_map/ppermute | solution.py:314
  245.3 67.9 %collective-permute-start.5 = (f32[128,4096]{1,0:T(8,128)}, f32[128,4096]{1,0:T(8,128)}, u32[]{:S(2)}, u32[]{:S(2)}) collective-permute-start(f32[128,4096]{1,0:T(8,128)} %collective-permute-done.4.near_ref), channel_id=1, source_target_pairs={{0,1},{1,0},{2,3},{3,2},{4,5},{5,4},{6,7},{7,6}} | collective-permute-start | bytes 6291464 | tf_op jit(solution)/shard_map/ppermute | solution.py:314
  260.7 79.6 %collective-permute-start.29 = (f32[256,512]{1,0:T(8,128)}, f32[256,512]{1,0:T(8,128)}, u32[]{:S(2)}, u32[]{:S(2)}) collective-permute-start(f32[256,512]{1,0:T(8,128)} %get-tuple-element.41), channel_id=1, source_target_pairs={{0,3},{1,2},{4,7},{5,6}} | collective-permute-start | bytes 1572872 | tf_op jit(solution)/shard_map/ppermute | solution.py:314
  262.8 79.0 %collective-permute-start.1 = (f32[128,4096]{1,0:T(8,128)}, f32[128,4096]{1,0:T(8,128)S(1)}, u32[]{:S(2)}, u32[]{:S(2)}) collective-permute-start(f32[128,4096]{1,0:T(8,128)} %collective-permute-done.near_ref), channel_id=1, source_target_pairs={{0,1},{1,0},{2,3},{3,2},{4,5},{5,4},{6,7},{7,6}} | collective-permute-start | bytes 6291464 | tf_op jit(solution)/shard_map/ppermute | solution.py:314
  282.4 85.2 %collective-permute-start.24 = (f32[256,512]{1,0:T(8,128)}, f32[256,512]{1,0:T(8,128)S(1)}, u32[]{:S(2)}, u32[]{:S(2)}) collective-permute-start(f32[256,512]{1,0:T(8,128)} %get-tuple-element.43), channel_id=1, source_target_pairs={{0,2},{1,3},{4,6},{5,7}} | collective-permute-start | bytes 1572872 | tf_op jit(solution)/shard_map/ppermute | solution.py:314
  313.2 55.8 %collective-permute-start.25 = (f32[256,512]{1,0:T(8,128)}, f32[256,512]{1,0:T(8,128)S(1)}, u32[]{:S(2)}, u32[]{:S(2)}) collective-permute-start(f32[256,512]{1,0:T(8,128)} %get-tuple-element.42), channel_id=1, source_target_pairs={{0,3},{1,2},{4,7},{5,6}} | collective-permute-start | bytes 1572872 | tf_op jit(solution)/shard_map/ppermute | solution.py:314
  338.9 31.3 %collective-permute-start.20 = (f32[256,512]{1,0:T(8,128)}, f32[256,512]{1,0:T(8,128)S(1)}, u32[]{:S(2)}, u32[]{:S(2)}) collective-permute-start(f32[256,512]{1,0:T(8,128)} %get-tuple-element.45), channel_id=1, source_target_pairs={{0,2},{1,3},{4,6},{5,7}} | collective-permute-start | bytes 1572872 | tf_op jit(solution)/shard_map/ppermute | solution.py:314
  340.3 32.1 %collective-permute-start.30 = (f32[256,512]{1,0:T(8,128)}, f32[256,512]{1,0:T(8,128)}, u32[]{:S(2)}, u32[]{:S(2)}) collective-permute-start(f32[256,512]{1,0:T(8,128)} %collective-permute-done.28.xs_ref), channel_id=1, source_target_pairs={{0,4},{4,0},{1,5},{5,1},{2,6},{6,2},{3,7},{7,3}} | collective-permute-start | bytes 1572872 | tf_op jit(solution)/shard_map/ppermute | solution.py:314
  341.8 31.3 %collective-permute-start.31 = (f32[256,512]{1,0:T(8,128)}, f32[256,512]{1,0:T(8,128)}, u32[]{:S(2)}, u32[]{:S(2)}) collective-permute-start(f32[256,512]{1,0:T(8,128)} %collective-permute-done.29.xc_ref), channel_id=1, source_target_pairs={{0,4},{4,0},{1,5},{5,1},{2,6},{6,2},{3,7},{7,3}} | collective-permute-start | bytes 1572872 | tf_op jit(solution)/shard_map/ppermute | solution.py:314
  367.6 34.1 %collective-permute-start.21 = (f32[256,512]{1,0:T(8,128)}, f32[256,512]{1,0:T(8,128)S(1)}, u32[]{:S(2)}, u32[]{:S(2)}) collective-permute-start(f32[256,512]{1,0:T(8,128)} %get-tuple-element.44), channel_id=1, source_target_pairs={{0,3},{1,2},{4,7},{5,6}} | collective-permute-start | bytes 1572872 | tf_op jit(solution)/shard_map/ppermute | solution.py:314
  369.0 33.5 %collective-permute-start.16 = (f32[256,512]{1,0:T(8,128)}, f32[256,512]{1,0:T(8,128)S(1)}, u32[]{:S(2)}, u32[]{:S(2)}) collective-permute-start(f32[256,512]{1,0:T(8,128)} %get-tuple-element.47), channel_id=1, source_target_pairs={{0,2},{1,3},{4,6},{5,7}} | collective-permute-start | bytes 1572872 | tf_op jit(solution)/shard_map/ppermute | solution.py:314
  370.3 33.5 %collective-permute-start.17 = (f32[256,512]{1,0:T(8,128)}, f32[256,512]{1,0:T(8,128)}, u32[]{:S(2)}, u32[]{:S(2)}) collective-permute-start(f32[256,512]{1,0:T(8,128)} %get-tuple-element.46), channel_id=1, source_target_pairs={{0,3},{1,2},{4,7},{5,6}} | collective-permute-start | bytes 1572872 | tf_op jit(solution)/shard_map/ppermute | solution.py:314
  372.4 32.1 %collective-permute-start.26 = (f32[256,512]{1,0:T(8,128)S(1)}, f32[256,512]{1,0:T(8,128)S(1)}, u32[]{:S(2)}, u32[]{:S(2)}) collective-permute-start(f32[256,512]{1,0:T(8,128)S(1)} %collective-permute-done.24.xs_ref), channel_id=1, source_target_pairs={{0,4},{4,0},{1,5},{5,1},{2,6},{6,2},{3,7},{7,3}} | collective-permute-start | bytes 1572872 | tf_op jit(solution)/shard_map/ppermute | solution.py:314
  373.1 32.7 %collective-permute-start.27 = (f32[256,512]{1,0:T(8,128)S(1)}, f32[256,512]{1,0:T(8,128)S(1)}, u32[]{:S(2)}, u32[]{:S(2)}) collective-permute-start(f32[256,512]{1,0:T(8,128)S(1)} %collective-permute-done.25.xc_ref), channel_id=1, source_target_pairs={{0,4},{4,0},{1,5},{5,1},{2,6},{6,2},{3,7},{7,3}} | collective-permute-start | bytes 1572872 | tf_op jit(solution)/shard_map/ppermute | solution.py:314
  401.7 32.1 %collective-permute-start.22 = (f32[256,512]{1,0:T(8,128)S(1)}, f32[256,512]{1,0:T(8,128)}, u32[]{:S(2)}, u32[]{:S(2)}) collective-permute-start(f32[256,512]{1,0:T(8,128)S(1)} %collective-permute-done.20.xs_ref), channel_id=1, source_target_pairs={{0,4},{4,0},{1,5},{5,1},{2,6},{6,2},{3,7},{7,3}} | collective-permute-start | bytes 1572872 | tf_op jit(solution)/shard_map/ppermute | solution.py:314
  402.4 31.4 %collective-permute-start.23 = (f32[256,512]{1,0:T(8,128)S(1)}, f32[256,512]{1,0:T(8,128)}, u32[]{:S(2)}, u32[]{:S(2)}) collective-permute-start(f32[256,512]{1,0:T(8,128)S(1)} %collective-permute-done.21.xc_ref), channel_id=1, source_target_pairs={{0,4},{4,0},{1,5},{5,1},{2,6},{6,2},{3,7},{7,3}} | collective-permute-start | bytes 1572872 | tf_op jit(solution)/shard_map/ppermute | solution.py:314
  403.8 58.1 %collective-permute-start.18 = (f32[256,512]{1,0:T(8,128)S(1)}, f32[256,512]{1,0:T(8,128)}, u32[]{:S(2)}, u32[]{:S(2)}) collective-permute-start(f32[256,512]{1,0:T(8,128)S(1)} %collective-permute-done.16.xs_ref), channel_id=1, source_target_pairs={{0,4},{4,0},{1,5},{5,1},{2,6},{6,2},{3,7},{7,3}} | collective-permute-start | bytes 1572872 | tf_op jit(solution)/shard_map/ppermute | solution.py:314
  404.5 57.3 %collective-permute-start.19 = (f32[256,512]{1,0:T(8,128)}, f32[256,512]{1,0:T(8,128)}, u32[]{:S(2)}, u32[]{:S(2)}) collective-permute-start(f32[256,512]{1,0:T(8,128)} %collective-permute-done.17.xc_ref), channel_id=1, source_target_pairs={{0,4},{4,0},{1,5},{5,1},{2,6},{6,2},{3,7},{7,3}} | collective-permute-start | bytes 1572872 | tf_op jit(solution)/shard_map/ppermute | solution.py:314
  405.8 83.2 %collective-permute-start.35 = (f32[2,256,512]{2,1,0:T(8,128)}, f32[2,256,512]{2,1,0:T(8,128)S(1)}, u32[]{:S(2)}, u32[]{:S(2)}) collective-permute-start(f32[2,256,512]{2,1,0:T(8,128)} %get-tuple-element.40), channel_id=1, source_target_pairs={{0,1},{1,0},{2,3},{3,2},{4,5},{5,4},{6,7},{7,6}} | collective-permute-start | bytes 3145736 | tf_op jit(solution)/shard_map/ppermute | solution.py:314
  433.8 55.2 %collective-permute-start.34 = (f32[2,256,512]{2,1,0:T(8,128)}, f32[2,256,512]{2,1,0:T(8,128)S(1)}, u32[]{:S(2)}, u32[]{:S(2)}) collective-permute-start(f32[2,256,512]{2,1,0:T(8,128)} %get-tuple-element.39), channel_id=1, source_target_pairs={{0,1},{1,0},{2,3},{3,2},{4,5},{5,4},{6,7},{7,6}} | collective-permute-start | bytes 3145736 | tf_op jit(solution)/shard_map/ppermute | solution.py:314
  461.2 27.8 %collective-permute-start.33 = (f32[2,256,512]{2,1,0:T(8,128)}, f32[2,256,512]{2,1,0:T(8,128)S(1)}, u32[]{:S(2)}, u32[]{:S(2)}) collective-permute-start(f32[2,256,512]{2,1,0:T(8,128)} %get-tuple-element.38), channel_id=1, source_target_pairs={{0,1},{1,0},{2,3},{3,2},{4,5},{5,4},{6,7},{7,6}} | collective-permute-start | bytes 3145736 | tf_op jit(solution)/shard_map/ppermute | solution.py:314
  (19 other events, 226.4 us)
where the time goes:
time: 527 us; the launch traced here: 518 us
  Pallas kernels  317 us (60%)
  waiting for transfers between devices  107 us (20%)
  starting transfers between devices  70.9 us (13%)
  local copies, waits for them, and re-layouts  12.5 us (2%)
  other arithmetic  10.3 us (2%)
    pallas_call x4, Pallas kernels, conv(): pl.pallas_call(conv_body, grid_spec=pltpu.PrefetchScalarGridSpec(num_scal...  109 us
    ppermute x36, waiting for transfers between devices, hop(): return lax.ppermute(x, axis, perm)  107 us
    pallas_call x1, Pallas kernels, compute(): pl.pallas_call(functools.partial(in_own_body, nt), grid_spec=pltpu.Prefet...  79.7 us
    ppermute x36, starting transfers between devices, hop(): return lax.ppermute(x, axis, perm)  70.9 us
    pallas_call x2, Pallas kernels, prev_b(): pl.pallas_call(functools.partial(prev_b_body, nt), grid_spec=pltpu.Prefet...  48.9 us
    pallas_call x2, Pallas kernels, prev_a(): pl.pallas_call(prev_a_body, grid_spec=pltpu.PrefetchScalarGridSpec(num_sc...  38.1 us
    pallas_call x1, Pallas kernels, compute(): pl.pallas_call(functools.partial(out_body, N_CHUNK), grid_spec=pltpu.Pref...  26 us
    pallas_call x1, Pallas kernels, compute(): pl.pallas_call(far_body, grid_spec=pltpu.PrefetchScalarGridSpec(num_scala...  15.4 us
  transfers between devices with their start and end apart: 36, of which 4 were waited for; matrix products, arithmetic and copies ran while one was open for 2% of the time, Pallas kernels for 56%

commit v1 on v0

--- a/solution.py
+++ b/solution.py
@@ -12,7 +12,8 @@
 BLK = 128
 TN = 512
 TC = 256
-N_CHUNK = 4
+N_PRE = 2
+MESH = pl.DeviceIdType.MESH
 
 
 def split_table(table):
@@ -165,40 +166,100 @@
                 g_ref[f, j, re], g_ref[f, j, im] = new_re, new_im
 
 
-def out_body(n_chunk, sc_ref, *refs):
-    keeps, parts = refs[:n_chunk], refs[n_chunk:2 * n_chunk]
-    wk_ref, wp_ref, u_ref, o_ref, lhs_k, lhs_p = refs[2 * n_chunk:]
-
+def out_body(sc_ref, keep_ref, part_ref, wk_ref, wp_ref, u_ref, o_ref, lhs_k, lhs_p):
     @pl.when(pl.program_id(0) == 0)
     def _():
-        n_seq, n_pos, nch = keeps[0].shape
-        for i in range(n_chunk):
-            cols = slice(i * nch, (i + 1) * nch)
-            lhs_k[:, cols] = keeps[i][...].reshape(n_seq * n_pos, nch)
-            lhs_p[:, cols] = parts[i][...].reshape(n_seq * n_pos, nch).astype(BF16)
+        rows = keep_ref.shape[0] * keep_ref.shape[1]
+        lhs_k[...] = keep_ref[...].reshape(rows, -1)
+        lhs_p[...] = part_ref[...].reshape(rows, -1).astype(BF16)
 
     acc = dot(lhs_k[...], wk_ref[...]) + dot(lhs_p[...], wp_ref[...])
     o_ref[...] = (u_ref[...].astype(F32) + acc.reshape(o_ref.shape)).astype(BF16)
 
 
-def conv_body(sc_ref, fwd6_ref, inv6_ref, x1_ref, v_ref, x2_ref, vhat, far_ref, sk1_ref, sk2_ref,
-              own1_ref, own2_ref, pf1_ref, pf2_ref, xs_ref, xc_ref, ys_ref, yc_ref,
-              keep_ref, send_ref, hparts, g1, g2, sp0, sp1, zp0, zp1, zv0, zv1, zh0, zh1, ybuf):
-    c, on_b, d = sc_ref[0], sc_ref[1] == 1, sc_ref[2]
+def conv_body(n_tile, fwd6_ref, inv6_ref, x1_ref, v_ref, x2_ref, vhat, far_ref, sk1_ref, sk2_ref,
+              f1_any, f2_any, pf1_any, pf2_any, xs_any, xc_any, ys_any, yc_any,
+              keep_ref, part_any, hparts, g1, g2, sp0, sp1, zp0, zp1, zv0, zv1, zh0, zh1, ybuf, land, sendbuf,
+              l_sem, x_send, x_recv, y_send, y_recv, p_send, p_recv):
+    t = pl.program_id(0)
+    sp, dp = lax.axis_index("sp"), lax.axis_index("dp")
+    c, d = lax.rem(sp, 2), dp
+    on_b = sp >= 2
     n_seq, nb = vhat.shape[0], vhat.shape[1]
     nbo = nb // 2
-    hk = own1_ref.shape[0] // BLK
+    half_w = n_tile * TC
+    hk = f1_any.shape[0] // BLK
     g, sparts, zparts, zval, zhat = (g1, g2), (sp0, sp1), (zp0, zp1), (zv0, zv1), (zh0, zh1)
 
-    @pl.when(on_b)
-    def _():
-        for ref, f, side in ((xs_ref, d, c), (xc_ref, d, 1 - c), (ys_ref, 1 - d, c), (yc_ref, 1 - d, 1 - c)):
-            split_blocks(ref, hparts.at[f], side * hk)
-
-    @pl.when(jnp.logical_not(on_b))
-    def _():
-        for ref, f, side in ((own1_ref, 0, c), (pf1_ref, 0, 1 - c), (own2_ref, 1, c), (pf2_ref, 1, 1 - c)):
-            split_blocks(ref, hparts.at[f], side * hk)
+    def cols(start):
+        return pl.ds(pl.multiple_of(start, TC), TC)
+
+    def fill(f, u, side, src, start):
+        return pltpu.make_async_copy(src.at[:, cols(start)], land.at[f, u, side], l_sem.at[f, u, side])
+
+    def over(src, u, k):
+        return pltpu.make_async_remote_copy(
+            src.at[:, cols(k * half_w + u * TC)], land.at[d, u, c], x_send.at[u, k], x_recv.at[u, c],
+            device_id=(dp, 2 + k), device_id_type=MESH)
+
+    def landed(u, side):
+        return pltpu.make_async_remote_copy(
+            land.at[d, u, side], land.at[d, u, side], x_send.at[u, side], x_recv.at[u, side],
+            device_id=(dp, sp), device_id_type=MESH)
+
+    def across(u, side, f):
+        return pltpu.make_async_remote_copy(
+            land.at[f, u, side], land.at[f, u, side], y_send.at[u, side], y_recv.at[u, side],
+            device_id=(1 - dp, sp), device_id_type=MESH)
+
+    def swap(u):
+        return pltpu.make_async_remote_copy(
+            sendbuf.at[lax.rem(u, 2)], part_any.at[:, :, cols(u * TC)], p_send.at[u], p_recv.at[u],
+            device_id=(dp, sp + 1 - 2 * c), device_id_type=MESH)
+
+    @pl.when(t == 0)
+    def _():
+        barrier = pltpu.get_barrier_semaphore()
+        other = sp + 1 - 2 * c
+        across_x, across_both = lax.rem(sp + 2, 4), lax.rem(other + 2, 4)
+        for peer in ((dp, other), (dp, across_x), (dp, across_both), (1 - dp, sp)):
+            pl.semaphore_signal(barrier, inc=1, device_id=peer, device_id_type=MESH)
+        pl.semaphore_wait(barrier, 4)
+
+        @pl.when(jnp.logical_not(on_b))
+        def _():
+            for which, src in ((0, f1_any), (1, f2_any)):
+                @pl.when(d == which)
+                def _():
+                    for u in range(N_PRE, n_tile):
+                        for k in range(2):
+                            over(src, u, k).start()
+            for u in range(n_tile):
+                for f, (own, part) in enumerate(((f1_any, pf1_any), (f2_any, pf2_any))):
+                    fill(f, u, c, own, c * half_w + u * TC).start()
+                    fill(f, u, 1 - c, part, u * TC).start()
+
+        @pl.when(on_b)
+        def _():
+            for u in range(N_PRE):
+                for f, (same, cross) in ((d, (xs_any, xc_any)), (1 - d, (ys_any, yc_any))):
+                    fill(f, u, c, same, u * TC).start()
+                    fill(f, u, 1 - c, cross, u * TC).start()
+
+    @pl.when(jnp.logical_or(jnp.logical_not(on_b), t < N_PRE))
+    def _():
+        for f in range(2):
+            for side in range(2):
+                fill(f, t, side, xs_any, 0).wait()
+
+    @pl.when(jnp.logical_and(on_b, t >= N_PRE))
+    def _():
+        for side in range(2):
+            across(t, side, 1 - d).wait_recv()
+
+    for f in range(2):
+        for side in range(2):
+            split_blocks(land.at[f, t, side], hparts.at[f], side * hk)
 
     def near_spectrum(f, j):
         g[f][j] = block_spectrum(fwd6_ref, hparts.at[f], j)
@@ -287,10 +348,45 @@
     for k in range(nbo):
         gate_two(1, k)
 
+    slot = lax.rem(t, 2)
+
+    @pl.when(t >= 2)
+    def _():
+        swap(t - 2).wait_send()
+
     for s in range(n_seq):
         for b in range(hk):
             keep_ref[s, b * BLK:(b + 1) * BLK] = ybuf[s, c * hk + b]
-            send_ref[s, b * BLK:(b + 1) * BLK] = ybuf[s, (1 - c) * hk + b].astype(F32)
+            sendbuf[slot, s, b * BLK:(b + 1) * BLK] = ybuf[s, (1 - c) * hk + b].astype(F32)
+
+    nxt = t + 2
+
+    @pl.when(jnp.logical_and(on_b, nxt < n_tile))
+    def _():
+        for side in range(2):
+            landed(nxt, side).wait_recv()
+            across(nxt, side, d).start()
+
+    swap(t).start()
+
+    @pl.when(t == n_tile - 1)
+    def _():
+        for u in (n_tile - 2, n_tile - 1):
+            swap(u).wait_send()
+        for u in range(n_tile):
+            swap(u).wait_recv()
+
+        @pl.when(on_b)
+        def _():
+            for u in range(N_PRE, n_tile):
+                for side in range(2):
+                    across(u, side, d).wait_send()
+
+        @pl.when(jnp.logical_not(on_b))
+        def _():
+            for u in range(N_PRE, n_tile):
+                for k in range(2):
+                    over(f1_any, u, k).wait_send()
 
 
 def params(mib=60):
@@ -333,7 +429,7 @@
         over = [hop(x, over_same) for x in pieces]
         over_part = [hop(x, partner) for x in over]
         u_part = [hop(x, partner) for x in pieces]
-        tail = jnp.concatenate([pieces[2 * s + 1][-8:] for s in range(n_seq)], axis=0)
+        tail = u_in[:, -8:].reshape(-1, width).astype(F32)
         u_tail = hop(tail, [(half_sp - 1, half_sp)]) + hop(tail, [(half_sp - 1, half_sp + 1)])
 
         mine, other = c * half_w, (1 - c) * half_w
@@ -342,15 +438,14 @@
             return lax.dynamic_slice(f, (0, start), (n_pos, half_w))
 
         f_part = [hop(chan_half(f, other), partner) for f in (filt_one, filt_two)]
-        f_link = jnp.where(dp == 0, filt_one, filt_two)
-        f_mine, f_other = chan_half(f_link, mine), chan_half(f_link, other)
-        nch = half_w // N_CHUNK
-        near = []
-        for j in range(N_CHUNK):
-            cols = slice(j * nch, (j + 1) * nch)
-            xs, xc = hop(f_mine[:, cols], over_same), hop(f_other[:, cols], over_cross)
-            ys, yc = hop(xs, swap_dp, "dp"), hop(xc, swap_dp, "dp")
-            near.append((xs, xc, ys, yc))
+        npre = N_PRE * TC
+
+        def pre(start):
+            f_link = [lax.dynamic_slice(f, (0, start), (n_pos, npre)) for f in (filt_one, filt_two)]
+            return jnp.where(dp == 0, *f_link)
+
+        xs, xc = hop(pre(mine), over_same), hop(pre(other), over_cross)
+        ys, yc = hop(xs, swap_dp, "dp"), hop(xc, swap_dp, "dp")
 
         bias = b_in.reshape(1, -1)
         nt = half_w // TN
@@ -474,62 +569,58 @@
             name="far_spectrum",
         )(scalars, fwd6, filt_one, filt_two, *f_part)
 
-        tiles = nch // TC
-        ht = half_w // TC
+        n_tile = half_w // TC
         q2 = q2.reshape(n_seq, nbo, BLK, half_w)
 
-        def conv(j, xs, xc, ys, yc):
-            base = j * tiles
-
-            def col4(shape, first):
-                return pl.BlockSpec(shape + (TC,), lambda t, sc: (0, 0, 0, first + base + t))
-
-            chan = pl.BlockSpec((1, TC), lambda t, sc: (0, sc[0] * ht + base + t))
-            own_f = pl.BlockSpec((n_pos, TC), lambda t, sc: (0, sc[0] * ht + base + t))
-            part_f = pl.BlockSpec((n_pos, TC), lambda t, sc: (0, base + t))
-            local = pl.BlockSpec((n_pos, TC), lambda t, sc: (0, t))
-            return pl.pallas_call(
-                conv_body,
-                grid_spec=pltpu.PrefetchScalarGridSpec(
-                    num_scalar_prefetch=1,
-                    grid=(tiles,),
-                    in_specs=[
-                        fixed(fwd6.shape), fixed(inv6.shape),
-                        col4((n_seq, nb, BLK), 0), col4((n_seq, nb, BLK), ht), col4((n_seq, nbo, BLK), 0),
-                        col4((n_seq, nb, 2 * BLK), 0), col4((2, nbo, 2 * BLK), 0),
-                        chan, chan, own_f, own_f,
-                        part_f, part_f, local, local, local, local,
-                    ],
-                    out_specs=[pl.BlockSpec((n_seq, n_pos, TC), lambda t, sc: (0, 0, t))] * 2,
-                    scratch_shapes=[
-                        pltpu.VMEM((2, nbo, 3, BLK, TC), BF16),
-                        *[pltpu.VMEM((nbo + 1, 2 * BLK, TC), F32)] * 2,
-                        *[pltpu.VMEM((nb, 3, 2 * BLK, TC), BF16)] * n_seq,
-                        *[pltpu.VMEM((nb, 3, BLK, TC), BF16)] * n_seq,
-                        *[pltpu.VMEM((nb, BLK, TC), F32)] * n_seq,
-                        *[pltpu.VMEM((nb, 2 * BLK, TC), F32)] * n_seq,
-                        pltpu.VMEM((n_seq, nbo, BLK, TC), BF16),
-                    ],
-                ),
-                out_shape=[jax.ShapeDtypeStruct((n_seq, n_pos, nch), BF16), jax.ShapeDtypeStruct((n_seq, n_pos, nch), F32)],
-                compiler_params=params(),
-                cost_estimate=cost(24e9 / N_CHUNK, 8e7 / N_CHUNK),
-                name="long_conv",
-            )(scalars, fwd6, inv6, q, q, q2, vhat, far, skip_one.reshape(1, -1), skip_two.reshape(1, -1),
-              filt_one, filt_two, *f_part, xs, xc, ys, yc)
-
-        keeps, parts = [], []
-        for j in range(N_CHUNK):
-            keep, send = conv(j, *near[j])
-            keeps.append(keep)
-            parts.append(hop(send, partner))
+        def col4(shape, first):
+            return pl.BlockSpec(shape + (TC,), lambda t: (0, 0, 0, first + t))
+
+        def my_half(x):
+            return lax.dynamic_slice(x, (mine,), (half_w,)).reshape(1, -1)
+
+        chan = pl.BlockSpec((1, TC), lambda t: (0, t))
+        keep, part = pl.pallas_call(
+            functools.partial(conv_body, n_tile),
+            grid_spec=pltpu.PrefetchScalarGridSpec(
+                num_scalar_prefetch=0,
+                grid=(n_tile,),
+                in_specs=[
+                    fixed(fwd6.shape), fixed(inv6.shape),
+                    col4((n_seq, nb, BLK), 0), col4((n_seq, nb, BLK), n_tile), col4((n_seq, nbo, BLK), 0),
+                    col4((n_seq, nb, 2 * BLK), 0), col4((2, nbo, 2 * BLK), 0), chan, chan,
+                    *[any_spec] * 8,
+                ],
+                out_specs=[pl.BlockSpec((n_seq, n_pos, TC), lambda t: (0, 0, t)), any_spec],
+                scratch_shapes=[
+                    pltpu.VMEM((2, nbo, 3, BLK, TC), BF16),
+                    *[pltpu.VMEM((nbo + 1, 2 * BLK, TC), F32)] * 2,
+                    *[pltpu.VMEM((nb, 3, 2 * BLK, TC), BF16)] * n_seq,
+                    *[pltpu.VMEM((nb, 3, BLK, TC), BF16)] * n_seq,
+                    *[pltpu.VMEM((nb, BLK, TC), F32)] * n_seq,
+                    *[pltpu.VMEM((nb, 2 * BLK, TC), F32)] * n_seq,
+                    pltpu.VMEM((n_seq, nbo, BLK, TC), BF16),
+                    pltpu.VMEM((2, n_tile, 2, n_pos, TC), F32),
+                    pltpu.VMEM((2, n_seq, n_pos, TC), F32),
+                    pltpu.SemaphoreType.DMA((2, n_tile, 2)),
+                    *[pltpu.SemaphoreType.DMA((n_tile, 2))] * 4,
+                    *[pltpu.SemaphoreType.DMA((n_tile,))] * 2,
+                ],
+            ),
+            out_shape=[jax.ShapeDtypeStruct((n_seq, n_pos, half_w), BF16), jax.ShapeDtypeStruct((n_seq, n_pos, half_w), F32)],
+            compiler_params=pltpu.CompilerParams(
+                vmem_limit_bytes=60 << 20, dimension_semantics=("arbitrary",), collective_id=0, has_side_effects=True),
+            cost_estimate=cost(24e9, 8e7),
+            name="long_conv",
+        )(fwd6, inv6, q, q, q2, vhat, far, my_half(skip_one), my_half(skip_two), filt_one, filt_two, *f_part, xs, xc, ys, yc)
+
         return pl.pallas_call(
-            functools.partial(out_body, N_CHUNK),
+            out_body,
             grid_spec=pltpu.PrefetchScalarGridSpec(
                 num_scalar_prefetch=1,
                 grid=(wt,),
                 in_specs=[
-                    *[fixed((n_seq, n_pos, nch))] * (2 * N_CHUNK),
+                    fixed((n_seq, n_pos, half_w)),
+                    fixed((n_seq, n_pos, half_w)),
                     pl.BlockSpec((half_w, TN), lambda j, sc: (sc[0], j)),
                     pl.BlockSpec((half_w, TN), lambda j, sc: (1 - sc[0], j)),
                     pl.BlockSpec((n_seq, n_pos, TN), lambda j, sc: (0, 0, j)),
@@ -541,7 +632,7 @@
             compiler_params=params(),
             cost_estimate=cost(2 * n_seq * n_pos * width * width, 2 * width * width),
             name="out_proj",
-        )(scalars, *keeps, *parts, w_out, w_out, u_in)
+        )(scalars, keep, part, w_out, w_out, u_in)
 
     seq_spec = P("dp", "sp", None)
     filt_spec = P("sp", None)

time: 527 us -> 493 us (0.935)
  the two profiles are of different devices: /device:TPU:0 before, /device:TPU:7 now
where the time goes in v1:
time: 493 us; the launch traced here: 491 us
  Pallas kernels  311 us (63%)
  waiting for transfers between devices  123 us (25%)
  starting transfers between devices  35.4 us (7%)
  local copies, waits for them, and re-layouts  10.8 us (2%)
  other arithmetic  10.2 us (2%)
    ppermute x20, waiting for transfers between devices, hop(): return lax.ppermute(x, axis, perm)  123 us
    pallas_call x1, Pallas kernels, compute(): pl.pallas_call(functools.partial(conv_body, n_tile), grid_spec=pltpu.Pref...  103 us
    pallas_call x1, Pallas kernels, compute(): pl.pallas_call(functools.partial(in_own_body, nt), grid_spec=pltpu.Prefet...  79.7 us
    pallas_call x2, Pallas kernels, prev_b(): pl.pallas_call(functools.partial(prev_b_body, nt), grid_spec=pltpu.Prefet...  49 us
    pallas_call x2, Pallas kernels, prev_a(): pl.pallas_call(prev_a_body, grid_spec=pltpu.PrefetchScalarGridSpec(num_sc...  38.1 us
    ppermute x20, starting transfers between devices, hop(): return lax.ppermute(x, axis, perm)  35.4 us
    pallas_call x1, Pallas kernels, compute(): pl.pallas_call(out_body, grid_spec=pltpu.PrefetchScalarGridSpec(num_scala...  26 us
    pallas_call x1, Pallas kernels, compute(): pl.pallas_call(far_body, grid_spec=pltpu.PrefetchScalarGridSpec(num_scala...  15.3 us
  transfers between devices with their start and end apart: 20, of which 4 were waited for; matrix products, arithmetic and copies ran while one was open for 2% of the time, Pallas kernels for 37%

profile of v1, /device:TPU:7, one launch (start us, length us, event | category | flops | bytes accessed | tf_op | source)
XLA Modules:
  0.0 491.0 jit_solution(18137505188264081960)
XLA Ops:
  0.0 2.7 slice_bitcast_fusion
  2.7 1.6 convert_element_type.20
  4.2 1.5 convert_element_type.21
  5.8 1.5 convert_element_type.22
  7.3 1.5 convert_element_type.23
  9.5 1.7 dynamic-slice_select_fusion
  11.2 1.3 collective-permute-start.16
  14.2 1.3 collective-permute-start.13
  15.5 14.8 %collective-permute-start.9 = (f32[128,4096]{1,0:T(8,128)}, f32[128,4096]{1,0:T(8,128)}, u32[]{:S(2)}, u32[]{:S(2)}) collective-permute-start(f32[128,4096]{1,0:T(8,128)} %convert_element_type.21), channel_id=1, source_target_pairs={{0,1},{1,0},{2,3},{3,2},{4,5},{5,4},{6,7},{7,6}} | collective-permute-start | bytes 6291464 | tf_op jit(solution)/shard_map/ppermute | solution.py:410
  30.3 2.1 collective-permute-done.13
  32.4 1.3 collective-permute-start.6
  33.7 1.3 collective-permute-start.4
  35.0 1.3 collective-permute-start.2
  38.2 3.3 constant_dynamic-slice_fusion.1
  41.6 1.5 constant_dynamic-slice_fusion
  43.8 1.3 collective-permute-start
  45.6 35.7 %collective-permute-done.6.near_ref = f32[128,4096]{1,0:T(8,128)} collective-permute-done((f32[128,4096]{1,0:T(8,128)}, f32[128,4096]{1,0:T(8,128)}, u32[]{:S(2)}, u32[]{:S(2)}) %collective-permute-start.6) | collective-permute-done | bytes 2097184 | tf_op jit(solution)/shard_map/ppermute | solution.py:410
  81.3 2.3 collective-permute-start.15
  83.6 42.6 %collective-permute-done.4.near_ref = f32[128,4096]{1,0:T(8,128)} collective-permute-done((f32[128,4096]{1,0:T(8,128)}, f32[128,4096]{1,0:T(8,128)}, u32[]{:S(2)}, u32[]{:S(2)}) %collective-permute-start.4) | collective-permute-done | bytes 2097184 | tf_op jit(solution)/shard_map/ppermute | solution.py:410
  126.3 2.3 collective-permute-start.7
  128.6 42.6 %collective-permute-done.2.near_ref = f32[128,4096]{1,0:T(8,128)} collective-permute-done((f32[128,4096]{1,0:T(8,128)}, f32[128,4096]{1,0:T(8,128)}, u32[]{:S(2)}, u32[]{:S(2)}) %collective-permute-start.2) | collective-permute-done | bytes 2097184 | tf_op jit(solution)/shard_map/ppermute | solution.py:410
  171.2 2.3 collective-permute-start.3
  173.5 79.7 %in_own.1 = (bf16[2,8,128,4096]{3,2,1,0:T(8,128)(2,1)}, bf16[2,512,2048]{2,1,0:T(8,128)(2,1)}, f32[2,8,256,2048]{3,2,1,0:T(8,128)}) custom-call(s32[3]{0:T(128)} %pad_add_fusion.sc_ref, bf16[256,384]{1,0:T(8,128)(2,1)} %constant.34.clone.fwd3_ref, bf16[2,256,4096]{2,1,0:T(8,128)(2,1)} %u_ref.1, f32[128,4096]{1,0:T(8,128)} %collective-permute-done.8.pa_ref, ...), custom_call_target="tpu_custom_call" | custom-call | flops 51539607552 | bytes 50331648 | tf_op jit(solution)/shard_map/in_own/pallas_call | solution.py:464
  253.3 1.5 collective-permute-start.17
  254.8 15.3 %far_spectrum.1.far_ref = f32[2,4,256,2048]{3,2,1,0:T(8,128)} custom-call(s32[3]{0:T(128)} %pad_add_fusion.sc_ref, bf16[256,768]{1,0:T(8,128)(2,1)} %constant.35.clone.fwd6_ref, f32[256,4096]{1,0:T(8,128)} %f1_any.1, f32[256,4096]{1,0:T(8,128)} %f2_any.1, f32[256,2048]{1,0:T(8,128)} %copy-done.1, f32[256,2048]{1,0:T(8,128)} %collective-permute-done.15.pf2_ref.pf2_any), custom_call_target="tpu_custom_call" | custom-call | flops 6000000000 | bytes 30000000 | tf_op jit(solution)/shard_map/far_spectrum/pallas_call | solution.py:551
  272.6 19.1 %prev_a.3.pa_ref = bf16[256,4096]{1,0:T(8,128)(2,1)} custom-call(s32[3]{0:T(128)} %pad_add_fusion.sc_ref, f32[128,4096]{1,0:T(8,128)} %collective-permute-done.6.near_ref, f32[128,4096]{1,0:T(8,128)} %collective-permute-done.7.far_ref, bf16[4096,12288]{1,0:T(8,128)(2,1)} %w_ref.9, f32[1,12288]{1,0:T(1,128)} %bitcast.20), custom_call_target="tpu_custom_call" | custom-call | flops 8589934592 | bytes 33554432 | tf_op jit(solution)/shard_map/prev_a/pallas_call | solution.py:495
  291.7 19.0 %prev_a.2.pa_ref = bf16[256,4096]{1,0:T(8,128)(2,1)} custom-call(s32[3]{0:T(128)} %pad_add_fusion.sc_ref, f32[128,4096]{1,0:T(8,128)} %collective-permute-done.2.near_ref, f32[128,4096]{1,0:T(8,128)} %collective-permute-done.3.far_ref, bf16[4096,12288]{1,0:T(8,128)(2,1)} %w_ref.9, f32[1,12288]{1,0:T(1,128)} %bitcast.21), custom_call_target="tpu_custom_call" | custom-call | flops 8589934592 | bytes 33554432 | tf_op jit(solution)/shard_map/prev_a/pallas_call | solution.py:495
  310.7 24.5 %prev_b.2 = (bf16[2,8,128,4096]{3,2,1,0:T(8,128)(2,1)}, f32[2,8,256,2048]{3,2,1,0:T(8,128)}) custom-call(s32[3]{0:T(128)} %pad_add_fusion.sc_ref, bf16[256,384]{1,0:T(8,128)(2,1)} %constant.34.clone.fwd3_ref, f32[128,4096]{1,0:T(8,128)} %collective-permute-done.4.near_ref, ...), custom_call_target="tpu_custom_call", output_to_operand_aliasing={{0}: (8, {}), {1}: (9, {})} | custom-call | flops 8589934592 | bytes 33554432 | tf_op jit(solution)/shard_map/prev_b/pallas_call | solution.py:517
  335.2 1.4 copy-done.2
  336.6 24.5 %prev_b.3 = (bf16[2,8,128,4096]{3,2,1,0:T(8,128)(2,1)}, f32[2,8,256,2048]{3,2,1,0:T(8,128)}) custom-call(s32[3]{0:T(128)} %pad_add_fusion.sc_ref, bf16[256,384]{1,0:T(8,128)(2,1)} %constant.34.clone.fwd3_ref, f32[128,4096]{1,0:T(8,128)} %collective-permute-done.near_ref, f32[128,4096]{1,0:T(8,128)} %copy-done.2, ...), custom_call_target="tpu_custom_call", output_to_operand_aliasing={{0}: (8, {}), {1}: (9, {})} | custom-call | flops 8589934592 | bytes 33554432 | tf_op jit(solution)/shard_map/prev_b/pallas_call | solution.py:517
  361.9 103.1 %long_conv.1 = (bf16[2,256,2048]{2,1,0:T(8,128)(2,1)}, f32[2,256,2048]{2,1,0:T(8,128)}) custom-call(bf16[256,768]{1,0:T(8,128)(2,1)} %constant.35.clone.fwd6_ref, bf16[128,1536]{1,0:T(8,128)(2,1)} %constant.36.clone.inv6_ref, bf16[2,8,128,4096]{3,2,1,0:T(8,128)(2,1)} %get-tuple-element.24.x1_ref.v_ref, ...), custom_call_target="tpu_custom_call" | custom-call | flops 24000000000 | bytes 80000000 | tf_op jit(solution)/shard_map/long_conv/pallas_call | solution.py:582
  465.0 26.0 %out_proj.1 = bf16[2,256,4096]{2,1,0:T(8,128)(2,1)} custom-call(s32[3]{0:T(128)} %pad_add_fusion.sc_ref, bf16[2,256,2048]{2,1,0:T(8,128)(2,1)} %get-tuple-element.27.keep_ref, f32[2,256,2048]{2,1,0:T(8,128)} %get-tuple-element.28.part_ref, bf16[4096,4096]{1,0:T(8,128)(2,1)} %wp_ref.1, bf16[4096,4096]{1,0:T(8,128)(2,1)} %wp_ref.1, bf16[2,256,4096]{2,1,0:T(8,128)(2,1)} %u_ref.1), custom_call_target="tpu_custom_call" | custom-call | flops 17179869184 | bytes 33554432 | tf_op jit(solution)/shard_map/out_proj/pallas_call | solution.py:616
  (45 shorter events, 8.8 us)
Async XLA Ops:
  8.8 27.5 %copy-start.6 = (f32[4096]{0:T(1024)S(1)}, f32[4096]{0:T(1024)}, u32[]{:S(2)}) copy-start(f32[4096]{0:T(1024)} %param.17) | copy-start | bytes 49156
  8.8 28.1 %copy-start.7 = (f32[4096]{0:T(1024)S(1)}, f32[4096]{0:T(1024)}, u32[]{:S(2)}) copy-start(f32[4096]{0:T(1024)} %param.18) | copy-start | bytes 49156
  8.8 24.9 %collective-permute-start.11 = (f32[128,4096]{1,0:T(8,128)}, f32[128,4096]{1,0:T(8,128)}, u32[]{:S(2)}, u32[]{:S(2)}) collective-permute-start(f32[128,4096]{1,0:T(8,128)} %convert_element_type.23), channel_id=1, source_target_pairs={{0,1},{1,0},{2,3},{3,2},{4,5},{5,4},{6,7},{7,6}} | collective-permute-start | bytes 6291464 | tf_op jit(solution)/shard_map/ppermute | solution.py:410
  9.5 25.5 %collective-permute-start.10 = (f32[128,4096]{1,0:T(8,128)}, f32[128,4096]{1,0:T(8,128)}, u32[]{:S(2)}, u32[]{:S(2)}) collective-permute-start(f32[128,4096]{1,0:T(8,128)} %convert_element_type.22), channel_id=1, source_target_pairs={{0,1},{1,0},{2,3},{3,2},{4,5},{5,4},{6,7},{7,6}} | collective-permute-start | bytes 6291464 | tf_op jit(solution)/shard_map/ppermute | solution.py:410
  11.2 21.2 %collective-permute-start.16 = (f32[256,512]{1,0:T(8,128)S(1)}, f32[256,512]{1,0:T(8,128)S(1)}, u32[]{:S(2)}, u32[]{:S(2)}) collective-permute-start(f32[256,512]{1,0:T(8,128)S(1)} %get-tuple-element.30), channel_id=1, source_target_pairs={{0,2},{1,3},{4,6},{5,7}} | collective-permute-start | bytes 1572872 | tf_op jit(solution)/shard_map/ppermute | solution.py:410
  13.5 2.0 collective-permute-start.12
  14.2 18.2 %collective-permute-start.13 = (f32[16,4096]{1,0:T(8,128)S(1)}, f32[16,4096]{1,0:T(8,128)S(1)}, u32[]{:S(2)}, u32[]{:S(2)}) collective-permute-start(f32[16,4096]{1,0:T(8,128)S(1)} %bitcast_convert_fusion), channel_id=1, source_target_pairs={{1,3},{5,7}} | collective-permute-start | bytes 786440 | tf_op jit(solution)/shard_map/ppermute | solution.py:410
  15.5 28.3 %collective-permute-start.9 = (f32[128,4096]{1,0:T(8,128)}, f32[128,4096]{1,0:T(8,128)}, u32[]{:S(2)}, u32[]{:S(2)}) collective-permute-start(f32[128,4096]{1,0:T(8,128)} %convert_element_type.21), channel_id=1, source_target_pairs={{0,1},{1,0},{2,3},{3,2},{4,5},{5,4},{6,7},{7,6}} | collective-permute-start | bytes 6291464 | tf_op jit(solution)/shard_map/ppermute | solution.py:410
  32.4 12.7 %collective-permute-start.8 = (f32[128,4096]{1,0:T(8,128)}, f32[128,4096]{1,0:T(8,128)}, u32[]{:S(2)}, u32[]{:S(2)}) collective-permute-start(f32[128,4096]{1,0:T(8,128)} %convert_element_type.20), channel_id=1, source_target_pairs={{0,1},{1,0},{2,3},{3,2},{4,5},{5,4},{6,7},{7,6}} | collective-permute-start | bytes 6291464 | tf_op jit(solution)/shard_map/ppermute | solution.py:410
  32.4 237.7 %copy-start.3 = (f32[256,512]{1,0:T(8,128)}, f32[256,512]{1,0:T(8,128)S(1)}, u32[]{:S(2)}) copy-start(f32[256,512]{1,0:T(8,128)S(1)} %collective-permute-done.16.xs_any) | copy-start | bytes 1572868
  32.4 48.9 %collective-permute-start.6 = (f32[128,4096]{1,0:T(8,128)}, f32[128,4096]{1,0:T(8,128)}, u32[]{:S(2)}, u32[]{:S(2)}) collective-permute-start(f32[128,4096]{1,0:T(8,128)} %convert_element_type.20), channel_id=1, source_target_pairs={{0,2},{1,3},{4,6},{5,7}} | collective-permute-start | bytes 6291464 | tf_op jit(solution)/shard_map/ppermute | solution.py:410
  33.7 92.5 %collective-permute-start.4 = (f32[128,4096]{1,0:T(8,128)}, f32[128,4096]{1,0:T(8,128)}, u32[]{:S(2)}, u32[]{:S(2)}) collective-permute-start(f32[128,4096]{1,0:T(8,128)} %convert_element_type.21), channel_id=1, source_target_pairs={{0,2},{1,3},{4,6},{5,7}} | collective-permute-start | bytes 6291464 | tf_op jit(solution)/shard_map/ppermute | solution.py:410
  35.0 136.2 %collective-permute-start.2 = (f32[128,4096]{1,0:T(8,128)}, f32[128,4096]{1,0:T(8,128)}, u32[]{:S(2)}, u32[]{:S(2)}) collective-permute-start(f32[128,4096]{1,0:T(8,128)} %convert_element_type.22), channel_id=1, source_target_pairs={{0,2},{1,3},{4,6},{5,7}} | collective-permute-start | bytes 6291464 | tf_op jit(solution)/shard_map/ppermute | solution.py:410
  38.2 3.3 copy-start
  43.8 226.6 %collective-permute-start = (f32[128,4096]{1,0:T(8,128)}, f32[128,4096]{1,0:T(8,128)}, u32[]{:S(2)}, u32[]{:S(2)}) collective-permute-start(f32[128,4096]{1,0:T(8,128)} %convert_element_type.23), channel_id=1, source_target_pairs={{0,2},{1,3},{4,6},{5,7}} | collective-permute-start | bytes 6291464 | tf_op jit(solution)/shard_map/ppermute | solution.py:410
  45.1 208.2 %collective-permute-start.14 = (f32[256,2048]{1,0:T(8,128)}, f32[256,2048]{1,0:T(8,128)S(1)}, u32[]{:S(2)}, u32[]{:S(2)}) collective-permute-start(f32[256,2048]{1,0:T(8,128)} %constant_dynamic-slice_fusion.1), channel_id=1, source_target_pairs={{0,1},{1,0},{2,3},{3,2},{4,5},{5,4},{6,7},{7,6}} | collective-permute-start | bytes 6291464 | tf_op jit(solution)/shard_map/ppermute | solution.py:410
  81.3 173.4 %collective-permute-start.15 = (f32[256,2048]{1,0:T(8,128)}, f32[256,2048]{1,0:T(8,128)}, u32[]{:S(2)}, u32[]{:S(2)}) collective-permute-start(f32[256,2048]{1,0:T(8,128)} %constant_dynamic-slice_fusion), channel_id=1, source_target_pairs={{0,1},{1,0},{2,3},{3,2},{4,5},{5,4},{6,7},{7,6}} | collective-permute-start | bytes 6291464 | tf_op jit(solution)/shard_map/ppermute | solution.py:410
  126.3 145.3 %collective-permute-start.7 = (f32[128,4096]{1,0:T(8,128)}, f32[128,4096]{1,0:T(8,128)}, u32[]{:S(2)}, u32[]{:S(2)}) collective-permute-start(f32[128,4096]{1,0:T(8,128)} %collective-permute-done.6.near_ref), channel_id=1, source_target_pairs={{0,1},{1,0},{2,3},{3,2},{4,5},{5,4},{6,7},{7,6}} | collective-permute-start | bytes 6291464 | tf_op jit(solution)/shard_map/ppermute | solution.py:410
  171.2 120.5 %collective-permute-start.3 = (f32[128,4096]{1,0:T(8,128)}, f32[128,4096]{1,0:T(8,128)}, u32[]{:S(2)}, u32[]{:S(2)}) collective-permute-start(f32[128,4096]{1,0:T(8,128)} %collective-permute-done.2.near_ref), channel_id=1, source_target_pairs={{0,1},{1,0},{2,3},{3,2},{4,5},{5,4},{6,7},{7,6}} | collective-permute-start | bytes 6291464 | tf_op jit(solution)/shard_map/ppermute | solution.py:410
  253.3 1.5 copy-start.1
  253.3 16.8 %collective-permute-start.17 = (f32[256,512]{1,0:T(8,128)S(1)}, f32[256,512]{1,0:T(8,128)S(1)}, u32[]{:S(2)}, u32[]{:S(2)}) collective-permute-start(f32[256,512]{1,0:T(8,128)S(1)} %get-tuple-element.29), channel_id=1, source_target_pairs={{0,3},{1,2},{4,7},{5,6}} | collective-permute-start | bytes 1572872 | tf_op jit(solution)/shard_map/ppermute | solution.py:410
  254.8 56.0 %collective-permute-start.5 = (f32[128,4096]{1,0:T(8,128)}, f32[128,4096]{1,0:T(8,128)}, u32[]{:S(2)}, u32[]{:S(2)}) collective-permute-start(f32[128,4096]{1,0:T(8,128)} %collective-permute-done.4.near_ref), channel_id=1, source_target_pairs={{0,1},{1,0},{2,3},{3,2},{4,5},{5,4},{6,7},{7,6}} | collective-permute-start | bytes 6291464 | tf_op jit(solution)/shard_map/ppermute | solution.py:410
  270.1 21.6 %copy-start.4 = (f32[256,512]{1,0:T(8,128)}, f32[256,512]{1,0:T(8,128)S(1)}, u32[]{:S(2)}) copy-start(f32[256,512]{1,0:T(8,128)S(1)} %collective-permute-done.17.xc_any) | copy-start | bytes 1572868
  270.1 91.0 %collective-permute-start.18 = (f32[256,512]{1,0:T(8,128)S(1)}, f32[256,512]{1,0:T(8,128)S(1)}, u32[]{:S(2)}, u32[]{:S(2)}) collective-permute-start(f32[256,512]{1,0:T(8,128)S(1)} %collective-permute-done.16.xs_any), channel_id=1, source_target_pairs={{0,4},{4,0},{1,5},{5,1},{2,6},{6,2},{3,7},{7,3}} | collective-permute-start | bytes 1572872 | tf_op jit(solution)/shard_map/ppermute | solution.py:410
  270.3 90.7 %collective-permute-start.19 = (f32[256,512]{1,0:T(8,128)S(1)}, f32[256,512]{1,0:T(8,128)}, u32[]{:S(2)}, u32[]{:S(2)}) collective-permute-start(f32[256,512]{1,0:T(8,128)S(1)} %collective-permute-done.17.xc_any), channel_id=1, source_target_pairs={{0,4},{4,0},{1,5},{5,1},{2,6},{6,2},{3,7},{7,3}} | collective-permute-start | bytes 1572872 | tf_op jit(solution)/shard_map/ppermute | solution.py:410
  271.6 63.6 %collective-permute-start.1 = (f32[128,4096]{1,0:T(8,128)}, f32[128,4096]{1,0:T(8,128)S(1)}, u32[]{:S(2)}, u32[]{:S(2)}) collective-permute-start(f32[128,4096]{1,0:T(8,128)} %collective-permute-done.near_ref), channel_id=1, source_target_pairs={{0,1},{1,0},{2,3},{3,2},{4,5},{5,4},{6,7},{7,6}} | collective-permute-start | bytes 6291464 | tf_op jit(solution)/shard_map/ppermute | solution.py:410
  335.2 1.4 copy-start.2
  361.1 0.8 copy-start.5
